TPU v7x, 128 devices: a whole 4x4x4 slice. The times are simulated.
128 devices in a mesh: row: 64 (over z, y, x), col: 2 (over core).
Axes of the slice: x: 4, y: 4, z: 4, core: 2. Of those that a mesh axis runs over, the one named last changes fastest.
Arguments:
- matrix: float32 [12288, 12288], P('row', 'col'), may hold values from -2 to 2, as said below
- diagonal: float32 [12288], P(('row', 'col')), may hold values from 1 to 6
- start: float32 [12288], P(('row', 'col')), may hold values from -6 to 6
Outputs:
- basis: float32 [4, 12288], P(None, ('row', 'col'))
- coefficients: float32 [2, 3], replicated
Inputs may be any that keep to these rules, and one draw needn't show every extreme that they name: matrix is exactly symmetric, its entries of order one over the square root of 12288.
All inputs are finite; a program needn't handle non-finite values.
Results may differ from a plain program's by a relative error of at most 0.0003.
Values sent between devices are 32-bit elements.
A program may use at most 64 MiB of HBM per device.

v0:
```python
import functools
import math

import jax
import jax.numpy as jnp
from jax import lax
from jax.sharding import Mesh
from jax.sharding import PartitionSpec as P

ITERS = 3
ROW = ("row_0", "row_1", "row_2")
ROW_COL = ("row_0", "row_1", "row_2", "col")


def over_axes(value, axes):
    return functools.reduce(lax.psum, axes, value)


def local(matrix, diagonal, start):
    rows_total = lax.axis_size(ROW)
    cols_total = lax.axis_size("col")
    tile_len = start.shape[0]
    full_dim = tile_len * rows_total * cols_total
    col_len = matrix.shape[1]
    col_idx = lax.axis_index("col")

    def apply_matrix(vector):
        gathered = lax.all_gather(vector, ROW_COL, axis=0, tiled=True)
        column = lax.dynamic_slice_in_dim(gathered, col_idx * col_len, col_len, 0)
        partial_value = jnp.dot(
            matrix, column, precision=lax.Precision.HIGHEST, preferred_element_type=jnp.float32
        )
        return (
            lax.psum_scatter(partial_value, "col", scatter_dimension=0, tiled=True)
            + diagonal * vector
        )

    start_sq = over_axes(jnp.sum(start * start), ROW_COL)
    current = start / jnp.sqrt(start_sq)
    basis_rows = jnp.zeros((ITERS + 1, tile_len), jnp.float32).at[0].set(current)
    alpha_list = []
    beta_list = []
    for iteration in range(ITERS):
        image = apply_matrix(current)
        local_intersect = jnp.dot(
            basis_rows, image, precision=lax.Precision.HIGHEST, preferred_element_type=jnp.float32
        )
        intersect, total_sq = (
            over_axes(local_intersect, ROW_COL),
            over_axes(jnp.sum(image * image), ROW_COL),
        )
        image = image - jnp.dot(
            intersect,
            basis_rows,
            precision=lax.Precision.HIGHEST,
            preferred_element_type=jnp.float32,
        )
        squared = total_sq - jnp.sum(intersect * intersect)
        beta_value = jnp.sqrt(squared)
        current = image / beta_value
        basis_rows = basis_rows.at[iteration + 1].set(current)
        alpha_list.append(intersect[iteration])
        beta_list.append(beta_value)
    coefficients = jnp.stack([jnp.stack(alpha_list), jnp.stack(beta_list)])
    return (basis_rows * jnp.float32(math.sqrt(full_dim)), coefficients)


def solution(mesh):
    split = Mesh(
        mesh.devices.reshape(4, 4, 4, mesh.shape["col"]), ("row_0", "row_1", "row_2", "col")
    )
    return jax.shard_map(
        local,
        mesh=split,
        in_specs=(P(ROW, "col"), P(ROW_COL), P(ROW_COL)),
        out_specs=(P(None, ROW_COL), P()),
        check_vma=False,
    )
```

profile of v0, /device:TPU:1, one launch (start us, length us, event | category | flops | bytes accessed | tf_op | source)
XLA Modules:
  0.0 365.5 jit_solution(11045711491770731486)
XLA Ops:
  0.6 0.0 copy-start.1
  0.6 0.0 copy-start
  0.7 1.3 multiply_reduce_fusion.6
  1.9 11.2 %psum.196 = f32[]{:T(128)} all-reduce(f32[]{:T(128)} %multiply_reduce_fusion.6), channel_id=1, replica_groups=mesh['row_0'=4,'row_1'=4,'row_2'=4,'col'=2] {'row_0'}, use_global_device_ids=true, to_apply=%region_1.0 | all-reduce | flops 1 | bytes 8 | tf_op jit(solution)/shard_map/psum | solution.py:16
  13.1 9.6 %psum.197 = f32[]{:T(128)} all-reduce(f32[]{:T(128)} %psum.196), channel_id=1, replica_groups=mesh['row_0'=4,'row_1'=4,'row_2'=4,'col'=2] {'row_1'}, use_global_device_ids=true, to_apply=%region_2.0 | all-reduce | flops 1 | bytes 8 | tf_op jit(solution)/shard_map/psum | solution.py:16
  22.7 9.1 %psum.198 = f32[]{:T(128)} all-reduce(f32[]{:T(128)} %psum.197), channel_id=1, replica_groups=mesh['row_0'=4,'row_1'=4,'row_2'=4,'col'=2] {'row_2'}, use_global_device_ids=true, to_apply=%region_3.0 | all-reduce | flops 1 | bytes 8 | tf_op jit(solution)/shard_map/psum | solution.py:16
  31.8 9.2 %psum.199 = f32[]{:T(128)} all-reduce(f32[]{:T(128)} %psum.198), channel_id=1, replica_groups=mesh['row_0'=4,'row_1'=4,'row_2'=4,'col'=2] {'col'}, use_global_device_ids=true, to_apply=%region_4.0 | all-reduce | flops 1 | bytes 8 | tf_op jit(solution)/shard_map/psum | solution.py:16
  41.7 0.8 fusion.17
  42.5 62.1 %all-reduce.1 = f32[12288]{0:T(1024)S(1)} all-reduce(f32[12288]{0:T(1024)S(1)} %get-tuple-element.80), channel_id=1, replica_groups=mesh['row_0'=4,'row_1'=4,'row_2'=4,'col'=2] {'row_0','row_1','row_2','col'}, use_global_device_ids=true, to_apply=%add.1 | all-reduce | flops 12288 | bytes 98304
  104.5 5.5 %fusion.18 = f32[1,192]{1,0:T(1,128)S(1)} fusion(f32[6144,1]{0,1:T(1,128)S(1)} %bitcast.75, f32[192,6144]{1,0:T(8,128)} %param.11), kind=kOutput, calls=%fused_computation.39 | convolution fusion | flops 14155776 | bytes 4743936 | tf_op jit(solution)/shard_map/dot_general | solution.py:30
  110.1 2.8 all-reduce.4
  112.8 0.0 copy-done.1
  112.8 0.6 dynamic-slice.31
  114.1 0.0 copy-done
  114.1 0.7 multiply_reduce_fusion.5
  114.8 0.1 convolution_bitcast_fusion.5
  114.9 8.6 %all-reduce.15 = (f32[4]{0:T(128)S(1)}, f32[]{:T(128)}) all-reduce(f32[4]{0:T(128)S(1)} %convolution_bitcast_fusion.5, f32[]{:T(128)} %get-tuple-element.78), channel_id=1, replica_groups=mesh['row_0'=4,'row_1'=4,'row_2'=4,'col'=2] {'row_0'}, use_global_device_ids=true, to_apply=%region_6.0 | all-reduce | flops 5 | bytes 40 | tf_op jit(solution)/shard_map/psum | solution.py:16
  123.5 7.3 %all-reduce.12 = (f32[4]{0:T(128)S(1)}, f32[]{:T(128)}) all-reduce(f32[4]{0:T(128)S(1)} %get-tuple-element.66, f32[]{:T(128)} %get-tuple-element.67), channel_id=1, replica_groups=mesh['row_0'=4,'row_1'=4,'row_2'=4,'col'=2] {'row_1'}, use_global_device_ids=true, to_apply=%region_7.0 | all-reduce | flops 5 | bytes 40 | tf_op jit(solution)/shard_map/psum | solution.py:16
  130.8 7.5 %all-reduce.9 = (f32[4]{0:T(128)S(1)}, f32[]{:T(128)}) all-reduce(f32[4]{0:T(128)S(1)} %get-tuple-element.60, f32[]{:T(128)} %get-tuple-element.61), channel_id=1, replica_groups=mesh['row_0'=4,'row_1'=4,'row_2'=4,'col'=2] {'row_2'}, use_global_device_ids=true, to_apply=%region_8.0 | all-reduce | flops 5 | bytes 40 | tf_op jit(solution)/shard_map/psum | solution.py:16
  138.3 9.1 %all-reduce.18 = (f32[4]{0:T(128)S(1)}, f32[]{:T(128)}) all-reduce(f32[4]{0:T(128)S(1)} %get-tuple-element.54, f32[]{:T(128)} %get-tuple-element.55), channel_id=1, replica_groups=mesh['row_0'=4,'row_1'=4,'row_2'=4,'col'=2] {'col'}, use_global_device_ids=true, to_apply=%region_9.0 | all-reduce | flops 5 | bytes 40 | tf_op jit(solution)/shard_map/psum | solution.py:16
  147.3 0.6 multiply_reduce_fusion.4
  149.3 0.1 fusion.1
  149.4 0.3 dynamic-update-slice.13
  149.7 62.6 %all-reduce.2 = f32[12288]{0:T(1024)S(1)} all-reduce(f32[12288]{0:T(1024)S(1)} %dynamic-update-slice.13), channel_id=1, replica_groups=mesh['row_0'=4,'row_1'=4,'row_2'=4,'col'=2] {'row_0','row_1','row_2','col'}, use_global_device_ids=true, to_apply=%add.2 | all-reduce | flops 12288 | bytes 98304
  212.3 5.5 %fusion.19 = f32[1,192]{1,0:T(1,128)S(1)} fusion(f32[6144,1]{0,1:T(1,128)S(1)} %bitcast.76, f32[192,6144]{1,0:T(8,128)} %param.11), kind=kOutput, calls=%fused_computation.40 | convolution fusion | flops 14155776 | bytes 4743936 | tf_op jit(solution)/shard_map/dot_general | solution.py:30
  217.8 2.8 all-reduce.5
  220.6 0.7 multiply_reduce_fusion.3
  221.3 0.1 convolution_bitcast_fusion.3
  221.4 7.9 %all-reduce.14 = (f32[4]{0:T(128)S(1)}, f32[]{:T(128)}) all-reduce(f32[4]{0:T(128)S(1)} %convolution_bitcast_fusion.3, f32[]{:T(128)} %get-tuple-element.76), channel_id=1, replica_groups=mesh['row_0'=4,'row_1'=4,'row_2'=4,'col'=2] {'row_0'}, use_global_device_ids=true, to_apply=%region_17.0 | all-reduce | flops 5 | bytes 40 | tf_op jit(solution)/shard_map/psum | solution.py:16
  229.4 8.0 %all-reduce.11 = (f32[4]{0:T(128)S(1)}, f32[]{:T(128)}) all-reduce(f32[4]{0:T(128)S(1)} %get-tuple-element.64, f32[]{:T(128)} %get-tuple-element.65), channel_id=1, replica_groups=mesh['row_0'=4,'row_1'=4,'row_2'=4,'col'=2] {'row_1'}, use_global_device_ids=true, to_apply=%region_18.0 | all-reduce | flops 5 | bytes 40 | tf_op jit(solution)/shard_map/psum | solution.py:16
  237.3 6.8 %all-reduce.8 = (f32[4]{0:T(128)S(1)}, f32[]{:T(128)}) all-reduce(f32[4]{0:T(128)S(1)} %get-tuple-element.58, f32[]{:T(128)} %get-tuple-element.59), channel_id=1, replica_groups=mesh['row_0'=4,'row_1'=4,'row_2'=4,'col'=2] {'row_2'}, use_global_device_ids=true, to_apply=%region_19.0 | all-reduce | flops 5 | bytes 40 | tf_op jit(solution)/shard_map/psum | solution.py:16
  244.2 9.1 %all-reduce.17 = (f32[4]{0:T(128)S(1)}, f32[]{:T(128)}) all-reduce(f32[4]{0:T(128)S(1)} %get-tuple-element.52, f32[]{:T(128)} %get-tuple-element.53), channel_id=1, replica_groups=mesh['row_0'=4,'row_1'=4,'row_2'=4,'col'=2] {'col'}, use_global_device_ids=true, to_apply=%region_20.0 | all-reduce | flops 5 | bytes 40 | tf_op jit(solution)/shard_map/psum | solution.py:16
  253.3 0.7 multiply_reduce_fusion.2
  255.4 0.1 fusion.3
  255.5 0.3 dynamic-update-slice.14
  255.8 63.2 %all-reduce.3 = f32[12288]{0:T(1024)S(1)} all-reduce(f32[12288]{0:T(1024)S(1)} %dynamic-update-slice.14), channel_id=1, replica_groups=mesh['row_0'=4,'row_1'=4,'row_2'=4,'col'=2] {'row_0','row_1','row_2','col'}, use_global_device_ids=true, to_apply=%add.3 | all-reduce | flops 12288 | bytes 98304
  319.0 5.5 %fusion.20 = f32[1,192]{1,0:T(1,128)S(1)} fusion(f32[6144,1]{0,1:T(1,128)S(1)} %bitcast.74, f32[192,6144]{1,0:T(8,128)} %param.11), kind=kOutput, calls=%fused_computation.41 | convolution fusion | flops 14155776 | bytes 4743936 | tf_op jit(solution)/shard_map/dot_general | solution.py:30
  324.5 3.0 all-reduce.6
  327.6 0.7 multiply_reduce_fusion.1
  328.3 0.1 convolution_bitcast_fusion.1
  328.4 7.1 %all-reduce.13 = (f32[4]{0:T(128)S(1)}, f32[]{:T(128)}) all-reduce(f32[4]{0:T(128)S(1)} %convolution_bitcast_fusion.1, f32[]{:T(128)} %get-tuple-element.74), channel_id=1, replica_groups=mesh['row_0'=4,'row_1'=4,'row_2'=4,'col'=2] {'row_0'}, use_global_device_ids=true, to_apply=%region_28.0 | all-reduce | flops 5 | bytes 40 | tf_op jit(solution)/shard_map/psum | solution.py:16
  335.5 8.7 %all-reduce.10 = (f32[4]{0:T(128)S(1)}, f32[]{:T(128)}) all-reduce(f32[4]{0:T(128)S(1)} %get-tuple-element.62, f32[]{:T(128)} %get-tuple-element.63), channel_id=1, replica_groups=mesh['row_0'=4,'row_1'=4,'row_2'=4,'col'=2] {'row_1'}, use_global_device_ids=true, to_apply=%region_29.0 | all-reduce | flops 5 | bytes 40 | tf_op jit(solution)/shard_map/psum | solution.py:16
  344.2 6.7 %all-reduce.7 = (f32[4]{0:T(128)S(1)}, f32[]{:T(128)}) all-reduce(f32[4]{0:T(128)S(1)} %get-tuple-element.56, f32[]{:T(128)} %get-tuple-element.57), channel_id=1, replica_groups=mesh['row_0'=4,'row_1'=4,'row_2'=4,'col'=2] {'row_2'}, use_global_device_ids=true, to_apply=%region_30.0 | all-reduce | flops 5 | bytes 40 | tf_op jit(solution)/shard_map/psum | solution.py:16
  350.9 8.8 %all-reduce.16 = (f32[4]{0:T(128)S(1)}, f32[]{:T(128)}) all-reduce(f32[4]{0:T(128)S(1)} %get-tuple-element.50, f32[]{:T(128)} %get-tuple-element.51), channel_id=1, replica_groups=mesh['row_0'=4,'row_1'=4,'row_2'=4,'col'=2] {'col'}, use_global_device_ids=true, to_apply=%region_31.0 | all-reduce | flops 5 | bytes 40 | tf_op jit(solution)/shard_map/psum | solution.py:16
  359.7 0.7 multiply_reduce_fusion
  361.7 0.6 slice.70
  362.3 0.6 slice.69
  362.9 1.3 maximum_bitcast_fusion
  364.1 0.6 pad_maximum_fusion
  364.7 0.1 fusion.6
  364.9 0.6 broadcast_multiply_fusion
  (10 shorter events, 0.1 us)
Async XLA Ops:
  0.6 112.2 %copy-start.1 = (u32[128]{0:T(128)S(1)}, u32[128]{0:T(128)}, u32[]{:S(2)}) copy-start(u32[128]{0:T(128)} %constant.143) | copy-start | bytes 1540
  0.6 113.4 %copy-start = (f32[96]{0:T(128)S(1)}, f32[96]{0:T(128)}, u32[]{:S(2)}) copy-start(f32[96]{0:T(128)} %param.12) | copy-start | bytes 1156
where the time goes:
time: 366 us; the launch traced here: 365 us
  blocking collectives  331 us (90%)
  matrix products  17.4 us (5%)
  other arithmetic  8.45 us (2%)
  between operations  6.08 us (2%)
    unnamed x6, blocking collectives  196 us
    psum x16, blocking collectives, over_axes(): return functools.reduce(lax.psum, axes, value)  135 us
    dot_general x3, matrix products, apply_matrix(): jnp.dot(matrix, column, precision=lax.Precision.HIGHEST, preferred_elemen...  16.6 us

commit v1 on v0

v1 whole, which is shorter than its diff:
```python
import math

import jax
import jax.numpy as jnp
from jax import lax
from jax.experimental import pallas as pl
from jax.experimental.pallas import tpu as pltpu
from jax.sharding import PartitionSpec as P

ITERS = 3
DIM = 12288
DEVICES = 128
ROWS = 192
COLS = 6144
TILE = 96
LANES = 128
PAIRS = 32
LOGICAL = pl.DeviceIdType.LOGICAL


def hops(step):
    return (0, 1, 2, 1)[step]


STEPS = sorted(
    (
        (i, j, k, m)
        for i in range(4)
        for j in range(4)
        for k in range(4)
        for m in range(2)
        if i or j or k or m
    ),
    key=lambda s: (-(hops(s[0]) + hops(s[1]) + hops(s[2])), s[3]),
)


def total(value):
    return jnp.sum(value, keepdims=True)


def kernel(matrix, diagonal, start, basis, coef, mat, frame, slots, x_rows, mat_sem, send_sem, recv_sem):
    row = lax.axis_index("row")
    col = lax.axis_index("col")
    me = row * 2 + col
    pair = row // 2
    odd = row % 2
    z, y, x = row // 16, (row // 4) % 4, row % 4
    z_part = [((z + i) % 4) * 32 for i in range(4)]
    y_part = [((y + i) % 4) * 8 for i in range(4)]
    x_part = [((x + i) % 4) * 2 for i in range(4)]
    c_part = [col, 1 - col]
    peers = [z_part[i] + y_part[j] + x_part[k] + c_part[m] for i, j, k, m in STEPS]

    barrier = pltpu.get_barrier_semaphore()
    for peer in peers:
        pl.semaphore_signal(barrier, inc=1, device_id=peer, device_id_type=LOGICAL)
    load = pltpu.make_async_copy(matrix, mat, mat_sem)
    load.start()

    lane = lax.broadcasted_iota(jnp.int32, (1, LANES), 1)

    def framed(part):
        wide = jnp.concatenate([part, jnp.zeros((1, LANES - TILE), jnp.float32)], axis=1)
        out = []
        for o in range(2):
            for c in range(2):
                offset = 64 * o + TILE * c
                shift = offset % LANES
                moved = pltpu.roll(wide, shift, 1) if shift else wide
                first, second = jnp.where(lane >= shift, moved, 0.0), jnp.where(lane < shift, moved, 0.0)
                zero = jnp.zeros_like(moved)
                out.append((zero, first) if offset >= LANES else (first, second))
        here = odd * 2 + col
        rows = []
        for h in range(2):
            pick = out[0][h]
            for n in range(1, 4):
                pick = jnp.where(here == n, out[n][h], pick)
            rows.append(pick)
        return jnp.concatenate(rows, axis=0)

    diag_frame = framed(diagonal[...])
    first_frame = framed(start[...])

    def exchange(k, value):
        frame[k] = value
        slots[k, me] = value
        for peer in peers:
            pltpu.make_async_remote_copy(
                src_ref=frame.at[k],
                dst_ref=slots.at[k, me],
                send_sem=send_sem.at[k],
                recv_sem=recv_sem.at[k],
                device_id=peer,
                device_id_type=LOGICAL,
            ).start()
        arrived = slots.at[k, 0 : DEVICES - 1]
        pltpu.make_async_copy(arrived, arrived, recv_sem.at[k]).wait()
        both = slots[k].reshape(PAIRS, 2, 2, 2, LANES)
        both = both[:, :, 0] + both[:, :, 1]
        even, uneven = both[:, 0], both[:, 1]
        return jnp.concatenate([even[:, 0:1], even[:, 1:2] + uneven[:, 0:1], uneven[:, 1:2]], axis=1)

    def rows_of(vector):
        return vector.reshape(3 * PAIRS, LANES)

    def multiply(vector):
        x_rows[...] = vector
        half = col * (3 * PAIRS // 2)

        def step(n, acc):
            value = x_rows[pl.ds(half + n, 1), :]
            wide = jnp.broadcast_to(value, (8, LANES))
            at = pl.multiple_of(n * LANES, LANES)
            return tuple(
                a + mat[8 * g : 8 * g + 8, pl.ds(at, LANES)] * wide for g, a in enumerate(acc)
            )

        acc = tuple(jnp.zeros((8, LANES), jnp.float32) for _ in range(ROWS // 8))
        acc = lax.fori_loop(0, COLS // LANES, step, acc, unroll=4)
        zero = jnp.zeros((8, LANES), jnp.float32)
        is_odd = odd == 1
        padded = [
            jnp.where(is_odd, acc[t - 8] if t >= 8 else zero, acc[t] if t < 24 else zero) for t in range(32)
        ]
        out = []
        for h in range(2):
            block = jnp.concatenate(padded[16 * h : 16 * h + 16], axis=0)
            out.append(jnp.sum(block.T, axis=0, keepdims=True))
        own = x_rows[pl.ds(pair * 3 + odd, 2), :]
        return jnp.concatenate(out, axis=0) + diag_frame * own

    def unframed(vector):
        x_rows[...] = vector
        own = x_rows[pl.ds(pair * 3 + odd, 2), :]
        first, second = own[0:1], own[1:2]
        pick = None
        for o in range(2):
            for c in range(2):
                offset = 64 * o + TILE * c
                shift = offset % LANES
                if offset >= LANES:
                    moved = pltpu.roll(second, LANES - shift, 1)
                elif shift:
                    moved = pltpu.roll(jnp.where(lane >= shift, first, second), LANES - shift, 1)
                else:
                    moved = first
                pick = moved if pick is None else jnp.where(odd * 2 + col == 2 * o + c, moved, pick)
        return pick[:, :TILE]

    pl.semaphore_wait(barrier, DEVICES - 1)

    scale = jnp.float32(math.sqrt(DIM))
    vector = rows_of(exchange(0, first_frame))
    vector = vector / jnp.sqrt(total(vector * vector))
    basis[0:1, :] = unframed(vector) * scale
    load.wait()
    known = [vector]
    alpha, beta = [], []
    for k in range(ITERS):
        image = rows_of(exchange(k + 1, multiply(known[-1])))
        dots = [total(q * image) for q in known]
        for h, q in zip(dots, known):
            image = image - h * q
        norm = jnp.sqrt(total(image * image))
        vector = image / norm
        basis[k + 1 : k + 2, :] = unframed(vector) * scale
        known.append(vector)
        alpha.append(dots[-1])
        beta.append(norm)
    coef[...] = jnp.concatenate(
        [jnp.concatenate(alpha, axis=1), jnp.concatenate(beta, axis=1)], axis=0
    )
    for k in range(ITERS + 1):
        sent = slots.at[k, 0 : DEVICES - 1]
        pltpu.make_async_copy(sent, sent, send_sem.at[k]).wait()


def solution(mesh):
    def local(matrix, diagonal, start):
        return pl.pallas_call(
            kernel,
            out_shape=(
                jax.ShapeDtypeStruct((ITERS + 1, TILE), jnp.float32),
                jax.ShapeDtypeStruct((2, ITERS), jnp.float32),
            ),
            in_specs=[
                pl.BlockSpec(memory_space=pl.ANY),
                pl.BlockSpec(memory_space=pltpu.VMEM),
                pl.BlockSpec(memory_space=pltpu.VMEM),
            ],
            out_specs=(pl.BlockSpec(memory_space=pltpu.VMEM), pl.BlockSpec(memory_space=pltpu.VMEM)),
            scratch_shapes=[
                pltpu.VMEM((ROWS, COLS), jnp.float32),
                pltpu.VMEM((ITERS + 1, 2, LANES), jnp.float32),
                pltpu.VMEM((ITERS + 1, DEVICES, 2, LANES), jnp.float32),
                pltpu.VMEM((3 * PAIRS, LANES), jnp.float32),
                pltpu.SemaphoreType.DMA,
                pltpu.SemaphoreType.DMA((ITERS + 1,)),
                pltpu.SemaphoreType.DMA((ITERS + 1,)),
            ],
            compiler_params=pltpu.CompilerParams(collective_id=0, has_side_effects=True),
        )(matrix, diagonal.reshape(1, TILE), start.reshape(1, TILE))

    return jax.shard_map(
        local,
        mesh=mesh,
        in_specs=(P("row", "col"), P(("row", "col")), P(("row", "col"))),
        out_specs=(P(None, ("row", "col")), P()),
        check_vma=False,
    )
```

time: 366 us -> 44 us (0.12)
  blocking collectives: 331 us -> 0 us
  Pallas kernels: 0 us -> 40.7 us
  matrix products: 17.4 us -> 0 us
  other arithmetic: 8.45 us -> 0 us
  between operations: 6.08 us -> 0.64 us
    unnamed x6 -> x0, blocking collectives: 196 us -> none
    psum x16 -> x0, blocking collectives: 135 us -> none  [over_axes(): return functools.reduce(lax.psum, axes, value)]
    pallas_call x0 -> x1, Pallas kernels: none -> 40.7 us  [local(): pl.pallas_call(kernel, out_shape=(jax.ShapeDtypeStruct((ITERS + 1, TILE),...]
    dot_general x9 -> x0, matrix products: 17.4 us -> none  [the longest x3 16.6 us: apply_matrix(): jnp.dot(matrix, column, precision=lax.Precision.HIGHEST, preferred_elemen...]
    reduce_sum x7 -> x0, other arithmetic: 5.24 us -> none  [the longest x3 2.02 us: local(): jnp.sum(image * image)]
where the time goes in v1:
time: 44 us; the launch traced here: 43.8 us
  Pallas kernels  40.7 us (93%)
  local copies, waits for them, and re-layouts  2.46 us (6%)
  between operations  0.64 us (1%)
    pallas_call x1, Pallas kernels, local(): pl.pallas_call(kernel, out_shape=(jax.ShapeDtypeStruct((ITERS + 1, TILE),...  40.7 us
    unnamed x2, local copies, waits for them, and re-layouts  2.46 us

profile of v1, /device:TPU:1, one launch (start us, length us, event | category | flops | bytes accessed | tf_op | source)
XLA Modules:
  0.0 43.8 jit_solution(16463300846596820323)
XLA Ops:
  0.6 40.7 %shard_map.50 = (f32[4,96]{1,0:T(4,128)}, f32[2,3]{1,0:T(2,128)}) custom-call(f32[192,6144]{1,0:T(8,128)} %matrix.1, f32[1,96]{1,0:T(1,128)} %bitcast.2, f32[1,96]{1,0:T(1,128)} %bitcast.3), custom_call_target="tpu_custom_call" | custom-call | tf_op jit(solution)/shard_map/pallas_call | solution.py:182
  41.3 1.2 %copy.7 = f32[4,96]{1,0:T(4,128)} copy(f32[4,96]{1,0:T(4,128)} %get-tuple-element.4) | data formatting | bytes 3072
  42.6 1.2 %copy.8 = f32[2,3]{1,0:T(2,128)} copy(f32[2,3]{1,0:T(2,128)} %get-tuple-element.5) | data formatting | bytes 48

commit v2 on v1

v2 whole, which is shorter than its diff:
```python
import math

import jax
import jax.numpy as jnp
from jax import lax
from jax.experimental import pallas as pl
from jax.experimental.pallas import tpu as pltpu
from jax.sharding import PartitionSpec as P

ITERS = 3
DIM = 12288
DEVICES = 128
ROWS = 192
COLS = 6144
TILE = 96
LANES = 128
PAIRS = 32
LOGICAL = pl.DeviceIdType.LOGICAL


def hops(step):
    return (0, 1, 2, 1)[step]


STEPS = sorted(
    (
        (i, j, k, m)
        for i in range(4)
        for j in range(4)
        for k in range(4)
        for m in range(2)
        if i or j or k or m
    ),
    key=lambda s: (-(hops(s[0]) + hops(s[1]) + hops(s[2])), s[3]),
)


def total(value):
    return jnp.sum(value, keepdims=True)


def kernel(matrix, diagonal, start, out, mat, small, frame, planes, x_rows, slots, mat_sem, small_sem, send_sem, recv_sem):
    row = lax.axis_index("row")
    col = lax.axis_index("col")
    pair = row // 2
    odd = row % 2
    here = odd * 2 + col
    z, y, x = row // 16, (row // 4) % 4, row % 4
    z_part = [((z + i) % 4) * 32 for i in range(4)]
    y_part = [((y + i) % 4) * 8 for i in range(4)]
    x_part = [((x + i) % 4) * 2 for i in range(4)]
    c_part = [col, 1 - col]
    peers = [z_part[i] + y_part[j] + x_part[k] + c_part[m] for i, j, k, m in STEPS]

    barrier = pltpu.get_barrier_semaphore()
    for peer in peers:
        pl.semaphore_signal(barrier, inc=1, device_id=peer, device_id_type=LOGICAL)
    load_start = pltpu.make_async_copy(start, small.at[0], small_sem.at[0])
    load_diag = pltpu.make_async_copy(diagonal, small.at[1], small_sem.at[1])
    load = pltpu.make_async_copy(matrix, mat, mat_sem)
    load_start.start()
    load_diag.start()
    load.start()

    lane = lax.broadcasted_iota(jnp.int32, (1, LANES), 1)

    def framed(part):
        wide = jnp.concatenate([part, jnp.zeros((1, LANES - TILE), jnp.float32)], axis=1)
        out = []
        for o in range(2):
            for c in range(2):
                offset = 64 * o + TILE * c
                shift = offset % LANES
                moved = pltpu.roll(wide, shift, 1) if shift else wide
                first, second = jnp.where(lane >= shift, moved, 0.0), jnp.where(lane < shift, moved, 0.0)
                zero = jnp.zeros_like(moved)
                out.append((zero, first) if offset >= LANES else (first, second))
        rows = []
        for h in range(2):
            pick = out[0][h]
            for n in range(1, 4):
                pick = jnp.where(here == n, out[n][h], pick)
            rows.append(pick)
        return rows

    def send(k, value):
        for h in range(2):
            frame[k, h] = value[h]
        for peer in peers:
            pltpu.make_async_remote_copy(
                src_ref=frame.at[k],
                dst_ref=planes.at[k, here, :, pl.ds(pair, 1), :],
                send_sem=send_sem.at[k],
                recv_sem=recv_sem.at[k],
                device_id=peer,
                device_id_type=LOGICAL,
            ).start()
        for h in range(2):
            planes[k, here, h, pl.ds(pair, 1), :] = value[h]

    def counted(sem):
        done = slots.at[:]
        return pltpu.make_async_copy(done, done, sem)

    def receive(k):
        counted(recv_sem.at[k]).wait()
        part = [planes[k, 0, h] + planes[k, 1, h] for h in range(2)]
        rest = [planes[k, 2, h] + planes[k, 3, h] for h in range(2)]
        rows = [part[0], part[1] + rest[0], rest[1]]
        for j in range(3):
            x_rows[j] = rows[j]
        return jnp.concatenate(rows, axis=0)

    def own_rows():
        return [x_rows[odd + h, pl.ds(pair, 1), :] for h in range(2)]

    def multiply(diag):
        own = own_rows()
        acc = [None] * (ROWS // 8)
        for n in range(COLS // LANES):
            value = x_rows[n % 3, pl.ds(col * (PAIRS // 2) + n // 3, 1), :]
            wide = jnp.broadcast_to(value, (8, LANES))
            for g in range(ROWS // 8):
                term = mat[8 * g : 8 * g + 8, n * LANES : (n + 1) * LANES] * wide
                acc[g] = term if n == 0 else acc[g] + term
        zero = jnp.zeros((8, LANES), jnp.float32)
        is_odd = odd == 1
        padded = [
            jnp.where(is_odd, acc[t - 8] if t >= 8 else zero, acc[t] if t < 24 else zero) for t in range(32)
        ]
        rows = []
        for h in range(2):
            block = jnp.concatenate(padded[16 * h : 16 * h + 16], axis=0)
            rows.append(jnp.sum(block.T, axis=0, keepdims=True) + diag[h] * own[h])
        return rows

    def unframed(first, second):
        pick = None
        for o in range(2):
            for c in range(2):
                offset = 64 * o + TILE * c
                shift = offset % LANES
                if offset >= LANES:
                    moved = pltpu.roll(second, LANES - shift, 1)
                elif shift:
                    moved = pltpu.roll(jnp.where(lane >= shift, first, second), LANES - shift, 1)
                else:
                    moved = first
                pick = moved if pick is None else jnp.where(here == 2 * o + c, moved, pick)
        return pick

    load_start.wait()
    first = framed(small[0])
    load_diag.wait()
    diag = framed(small[1])
    pl.semaphore_wait(barrier, DEVICES - 1)
    send(0, first)
    load.wait()

    scale = jnp.float32(math.sqrt(DIM))
    known, images, slices = [], [], []
    for k in range(ITERS + 1):
        vector = receive(k)
        own = unframed(*own_rows())
        if k < ITERS:
            image = multiply(diag)
        dots = [total(q * vector) for q in known]
        for h, q, s in zip(dots, known, slices):
            vector = vector - h * q
            own = own - h * s
        norm = jnp.sqrt(total(vector * vector))
        if k < ITERS:
            for h, f in zip(dots, images):
                image = [a - h * b for a, b in zip(image, f)]
            image = [a / norm for a in image]
            send(k + 1, image)
            images.append(image)
            known.append(vector / norm)
        own = own / norm
        slices.append(own)
        out[k : k + 1, :] = own * scale
        if k:
            column = lane == k - 1
            a_row = jnp.where(column, dots[-1], a_row if k > 1 else 0.0)
            b_row = jnp.where(column, norm, b_row if k > 1 else 0.0)
    out[4:5, :] = a_row
    out[5:6, :] = b_row
    for k in range(ITERS + 1):
        counted(send_sem.at[k]).wait()


def split_kernel(packed, basis, coef):
    basis[...] = packed[0:4, 0:TILE]
    coef[...] = packed[4:6, 0:ITERS]


def solution(mesh):
    vmem = pl.BlockSpec(memory_space=pltpu.VMEM)
    hbm = pl.BlockSpec(memory_space=pl.ANY)

    def local(matrix, diagonal, start):
        packed = pl.pallas_call(
            kernel,
            out_shape=pltpu.VMEM((8, LANES), jnp.float32),
            in_specs=[hbm, hbm, hbm],
            out_specs=vmem,
            scratch_shapes=[
                pltpu.VMEM((ROWS, COLS), jnp.float32),
                pltpu.VMEM((2, 1, TILE), jnp.float32),
                pltpu.VMEM((ITERS + 1, 2, 1, LANES), jnp.float32),
                pltpu.VMEM((ITERS + 1, 4, 2, PAIRS, LANES), jnp.float32),
                pltpu.VMEM((3, PAIRS, LANES), jnp.float32),
                pltpu.VMEM((DEVICES - 1, 2, LANES), jnp.float32),
                pltpu.SemaphoreType.DMA,
                pltpu.SemaphoreType.DMA((2,)),
                pltpu.SemaphoreType.DMA((ITERS + 1,)),
                pltpu.SemaphoreType.DMA((ITERS + 1,)),
            ],
            compiler_params=pltpu.CompilerParams(collective_id=0, has_side_effects=True),
        )(matrix, diagonal.reshape(1, TILE), start.reshape(1, TILE))
        return pl.pallas_call(
            split_kernel,
            out_shape=(
                jax.ShapeDtypeStruct((ITERS + 1, TILE), jnp.float32),
                jax.ShapeDtypeStruct((2, ITERS), jnp.float32),
            ),
            in_specs=[vmem],
            out_specs=(vmem, vmem),
        )(packed)

    return jax.shard_map(
        local,
        mesh=mesh,
        in_specs=(P("row", "col"), P(("row", "col")), P(("row", "col"))),
        out_specs=(P(None, ("row", "col")), P()),
        check_vma=False,
    )
```

time: 44 us -> 39.3 us (0.89)
  Pallas kernels: 40.7 us -> 37.9 us
  local copies, waits for them, and re-layouts: 2.46 us -> 0.58 us
    pallas_call x1 -> x2, Pallas kernels: 40.7 us -> 37.9 us  [the longest x1 36.7 us: local(): pl.pallas_call(kernel, out_shape=pltpu.VMEM((8, LANES), jnp.float32), in_...]
    unnamed x2, local copies, waits for them, and re-layouts: 2.46 us -> 0.58 us
where the time goes in v2:
time: 39.3 us; the launch traced here: 39.2 us
  Pallas kernels  37.9 us (96%)
  between operations  0.65 us (2%)
  local copies, waits for them, and re-layouts  0.58 us (1%)
    pallas_call x1, Pallas kernels, local(): pl.pallas_call(kernel, out_shape=pltpu.VMEM((8, LANES), jnp.float32), in_...  36.7 us
    pallas_call x1, Pallas kernels, local(): pl.pallas_call(split_kernel, out_shape=(jax.ShapeDtypeStruct((ITERS + 1,...  1.25 us

profile of v2, /device:TPU:1, one launch (start us, length us, event | category | flops | bytes accessed | tf_op | source)
XLA Modules:
  0.0 39.2 jit_solution(11105704666070239646)
XLA Ops:
  0.6 36.7 %shard_map.50.packed = f32[8,128]{1,0:T(8,128)S(1)} custom-call(f32[192,6144]{1,0:T(8,128)} %matrix.1, f32[1,96]{1,0:T(1,128)} %bitcast.2, f32[1,96]{1,0:T(1,128)} %bitcast.3), custom_call_target="tpu_custom_call" | custom-call | tf_op jit(solution)/shard_map/pallas_call | solution.py:202
  37.3 0.0 copy-start
  37.3 0.6 %copy-done = f32[8,128]{1,0:T(8,128)} copy-done((f32[8,128]{1,0:T(8,128)}, f32[8,128]{1,0:T(8,128)S(1)}, u32[]{:S(2)}) %copy-start) | copy-done | bytes 4120
  37.9 1.3 %shard_map.51 = (f32[4,96]{1,0:T(4,128)}, f32[2,3]{1,0:T(2,128)}) custom-call(f32[8,128]{1,0:T(8,128)} %copy-done), custom_call_target="tpu_custom_call" | custom-call | tf_op jit(solution)/shard_map/pallas_call | solution.py:221
Async XLA Ops:
  37.3 0.6 %copy-start = (f32[8,128]{1,0:T(8,128)}, f32[8,128]{1,0:T(8,128)S(1)}, u32[]{:S(2)}) copy-start(f32[8,128]{1,0:T(8,128)S(1)} %shard_map.50.packed) | copy-start | bytes 12292

commit v3 on v2

--- a/solution.py
+++ b/solution.py
@@ -226,7 +226,7 @@
             ),
             in_specs=[vmem],
             out_specs=(vmem, vmem),
-        )(packed)
+        )(pltpu.with_memory_space_constraint(packed, pltpu.VMEM))
 
     return jax.shard_map(
         local,

time: 39.3 us -> 38 us (0.967)
  Pallas kernels: 37.9 us -> 37.3 us
  local copies, waits for them, and re-layouts: 0.58 us -> 0 us
    pallas_call x1, Pallas kernels: 1.25 us -> 0.58 us  [local(): pl.pallas_call(split_kernel, out_shape=(jax.ShapeDtypeStruct((ITERS + 1,...]
    unnamed x2 -> x0, local copies, waits for them, and re-layouts: 0.58 us -> none
where the time goes in v3:
time: 38 us; the launch traced here: 37.9 us
  Pallas kernels  37.3 us (98%)
  between operations  0.64 us (2%)
    pallas_call x1, Pallas kernels, local(): pl.pallas_call(kernel, out_shape=pltpu.VMEM((8, LANES), jnp.float32), in_...  36.7 us

profile of v3, /device:TPU:1, one launch (start us, length us, event | category | flops | bytes accessed | tf_op | source)
XLA Modules:
  0.0 37.9 jit_solution(17081460520770217705)
XLA Ops:
  0.6 36.7 %shard_map.50.packed = f32[8,128]{1,0:T(8,128)S(1)} custom-call(f32[192,6144]{1,0:T(8,128)} %matrix.1, f32[1,96]{1,0:T(1,128)} %bitcast.2, f32[1,96]{1,0:T(1,128)} %bitcast.3), custom_call_target="tpu_custom_call" | custom-call | tf_op jit(solution)/shard_map/pallas_call | solution.py:202
  37.3 0.6 %shard_map.51 = (f32[4,96]{1,0:T(4,128)}, f32[2,3]{1,0:T(2,128)}) custom-call(f32[8,128]{1,0:T(8,128)S(1)} %shard_map.50.packed), custom_call_target="tpu_custom_call" | custom-call | tf_op jit(solution)/shard_map/pallas_call | solution.py:221

commit v4 on v3

--- a/solution.py
+++ b/solution.py
@@ -29,7 +29,7 @@
         for j in range(4)
         for k in range(4)
         for m in range(2)
-        if i or j or k or m
+        if i or j or k
     ),
     key=lambda s: (-(hops(s[0]) + hops(s[1]) + hops(s[2])), s[3]),
 )
@@ -45,12 +45,13 @@
     pair = row // 2
     odd = row % 2
     here = odd * 2 + col
+    slot = here * 2 * PAIRS + pair * 2
     z, y, x = row // 16, (row // 4) % 4, row % 4
     z_part = [((z + i) % 4) * 32 for i in range(4)]
     y_part = [((y + i) % 4) * 8 for i in range(4)]
     x_part = [((x + i) % 4) * 2 for i in range(4)]
-    c_part = [col, 1 - col]
-    peers = [z_part[i] + y_part[j] + x_part[k] + c_part[m] for i, j, k, m in STEPS]
+    peers = [z_part[i] + y_part[j] + x_part[k] + m for i, j, k, m in STEPS]
+    peers.append(row * 2 + 1 - col)
 
     barrier = pltpu.get_barrier_semaphore()
     for peer in peers:
@@ -85,18 +86,18 @@
 
     def send(k, value):
         for h in range(2):
-            frame[k, h] = value[h]
+            frame[k, h : h + 1, :] = value[h]
         for peer in peers:
             pltpu.make_async_remote_copy(
                 src_ref=frame.at[k],
-                dst_ref=planes.at[k, here, :, pl.ds(pair, 1), :],
+                dst_ref=planes.at[k, pl.ds(slot, 2), :],
                 send_sem=send_sem.at[k],
                 recv_sem=recv_sem.at[k],
                 device_id=peer,
                 device_id_type=LOGICAL,
             ).start()
         for h in range(2):
-            planes[k, here, h, pl.ds(pair, 1), :] = value[h]
+            planes[k, pl.ds(slot + h, 1), :] = value[h]
 
     def counted(sem):
         done = slots.at[:]
@@ -104,8 +105,11 @@
 
     def receive(k):
         counted(recv_sem.at[k]).wait()
-        part = [planes[k, 0, h] + planes[k, 1, h] for h in range(2)]
-        rest = [planes[k, 2, h] + planes[k, 3, h] for h in range(2)]
+        side = [
+            [planes[k, pl.ds(2 * PAIRS * n + h, PAIRS, stride=2), :] for h in range(2)] for n in range(4)
+        ]
+        part = [side[0][h] + side[1][h] for h in range(2)]
+        rest = [side[2][h] + side[3][h] for h in range(2)]
         rows = [part[0], part[1] + rest[0], rest[1]]
         for j in range(3):
             x_rows[j] = rows[j]
@@ -207,8 +211,8 @@
             scratch_shapes=[
                 pltpu.VMEM((ROWS, COLS), jnp.float32),
                 pltpu.VMEM((2, 1, TILE), jnp.float32),
-                pltpu.VMEM((ITERS + 1, 2, 1, LANES), jnp.float32),
-                pltpu.VMEM((ITERS + 1, 4, 2, PAIRS, LANES), jnp.float32),
+                pltpu.VMEM((ITERS + 1, 2, LANES), jnp.float32),
+                pltpu.VMEM((ITERS + 1, 8 * PAIRS, LANES), jnp.float32),
                 pltpu.VMEM((3, PAIRS, LANES), jnp.float32),
                 pltpu.VMEM((DEVICES - 1, 2, LANES), jnp.float32),
                 pltpu.SemaphoreType.DMA,

time: 38 us -> 38 us (level)
  no operation moved by 1% of the time
where the time goes in v4:
time: 38 us; the launch traced here: 37.9 us
  Pallas kernels  37.2 us (98%)
  between operations  0.64 us (2%)
    pallas_call x1, Pallas kernels, local(): pl.pallas_call(kernel, out_shape=pltpu.VMEM((8, LANES), jnp.float32), in_...  36.6 us

profile of v4, /device:TPU:1, one launch (start us, length us, event | category | flops | bytes accessed | tf_op | source)
XLA Modules:
  0.0 37.9 jit_solution(3010888741886712011)
XLA Ops:
  0.6 36.6 %shard_map.50.packed = f32[8,128]{1,0:T(8,128)S(1)} custom-call(f32[192,6144]{1,0:T(8,128)} %matrix.1, f32[1,96]{1,0:T(1,128)} %bitcast.2, f32[1,96]{1,0:T(1,128)} %bitcast.3), custom_call_target="tpu_custom_call" | custom-call | tf_op jit(solution)/shard_map/pallas_call | solution.py:206
  37.3 0.6 %shard_map.51 = (f32[4,96]{1,0:T(4,128)}, f32[2,3]{1,0:T(2,128)}) custom-call(f32[8,128]{1,0:T(8,128)S(1)} %shard_map.50.packed), custom_call_target="tpu_custom_call" | custom-call | tf_op jit(solution)/shard_map/pallas_call | solution.py:225

commit v5 on v4

--- a/solution.py
+++ b/solution.py
@@ -121,12 +121,13 @@
     def multiply(diag):
         own = own_rows()
         acc = [None] * (ROWS // 8)
-        for n in range(COLS // LANES):
-            value = x_rows[n % 3, pl.ds(col * (PAIRS // 2) + n // 3, 1), :]
-            wide = jnp.broadcast_to(value, (8, LANES))
-            for g in range(ROWS // 8):
-                term = mat[8 * g : 8 * g + 8, n * LANES : (n + 1) * LANES] * wide
-                acc[g] = term if n == 0 else acc[g] + term
+        for groups in (range(8), range(8, 16), range(16, 24)):
+            for n in range(COLS // LANES):
+                value = x_rows[n % 3, pl.ds(col * (PAIRS // 2) + n // 3, 1), :]
+                wide = jnp.broadcast_to(value, (8, LANES))
+                for g in groups:
+                    term = mat[8 * g : 8 * g + 8, n * LANES : (n + 1) * LANES] * wide
+                    acc[g] = term if n == 0 else acc[g] + term
         zero = jnp.zeros((8, LANES), jnp.float32)
         is_odd = odd == 1
         padded = [

time: 38 us -> 37.9 us (level)
  no operation moved by 1% of the time
where the time goes in v5:
time: 37.9 us; the launch traced here: 37.8 us
  Pallas kernels  37.2 us (98%)
  between operations  0.64 us (2%)
    pallas_call x1, Pallas kernels, local(): pl.pallas_call(kernel, out_shape=pltpu.VMEM((8, LANES), jnp.float32), in_...  36.6 us

profile of v5, /device:TPU:1, one launch (start us, length us, event | category | flops | bytes accessed | tf_op | source)
XLA Modules:
  0.0 37.8 jit_solution(2157289370524830294)
XLA Ops:
  0.6 36.6 %shard_map.50.packed = f32[8,128]{1,0:T(8,128)S(1)} custom-call(f32[192,6144]{1,0:T(8,128)} %matrix.1, f32[1,96]{1,0:T(1,128)} %bitcast.2, f32[1,96]{1,0:T(1,128)} %bitcast.3), custom_call_target="tpu_custom_call" | custom-call | tf_op jit(solution)/shard_map/pallas_call | solution.py:207
  37.2 0.6 %shard_map.51 = (f32[4,96]{1,0:T(4,128)}, f32[2,3]{1,0:T(2,128)}) custom-call(f32[8,128]{1,0:T(8,128)S(1)} %shard_map.50.packed), custom_call_target="tpu_custom_call" | custom-call | tf_op jit(solution)/shard_map/pallas_call | solution.py:226

commit v6 on v5

--- a/solution.py
+++ b/solution.py
@@ -179,6 +179,7 @@
                 image = [a - h * b for a, b in zip(image, f)]
             image = [a / norm for a in image]
             send(k + 1, image)
+            counted(send_sem.at[k]).wait()
             images.append(image)
             known.append(vector / norm)
         own = own / norm
@@ -190,8 +191,7 @@
             b_row = jnp.where(column, norm, b_row if k > 1 else 0.0)
     out[4:5, :] = a_row
     out[5:6, :] = b_row
-    for k in range(ITERS + 1):
-        counted(send_sem.at[k]).wait()
+    counted(send_sem.at[ITERS]).wait()
 
 
 def split_kernel(packed, basis, coef):

time: 37.9 us -> 37.9 us (level)
  no operation moved by 1% of the time
where the time goes in v6:
time: 37.9 us; the launch traced here: 37.8 us
  Pallas kernels  37.2 us (98%)
  between operations  0.64 us (2%)
    pallas_call x1, Pallas kernels, local(): pl.pallas_call(kernel, out_shape=pltpu.VMEM((8, LANES), jnp.float32), in_...  36.6 us

profile of v6, /device:TPU:1, one launch (start us, length us, event | category | flops | bytes accessed | tf_op | source)
XLA Modules:
  0.0 37.8 jit_solution(14278612226515929076)
XLA Ops:
  0.6 36.6 %shard_map.50.packed = f32[8,128]{1,0:T(8,128)S(1)} custom-call(f32[192,6144]{1,0:T(8,128)} %matrix.1, f32[1,96]{1,0:T(1,128)} %bitcast.2, f32[1,96]{1,0:T(1,128)} %bitcast.3), custom_call_target="tpu_custom_call" | custom-call | tf_op jit(solution)/shard_map/pallas_call | solution.py:207
  37.2 0.6 %shard_map.51 = (f32[4,96]{1,0:T(4,128)}, f32[2,3]{1,0:T(2,128)}) custom-call(f32[8,128]{1,0:T(8,128)S(1)} %shard_map.50.packed), custom_call_target="tpu_custom_call" | custom-call | tf_op jit(solution)/shard_map/pallas_call | solution.py:226

commit v7 on v6

--- a/solution.py
+++ b/solution.py
@@ -121,7 +121,7 @@
     def multiply(diag):
         own = own_rows()
         acc = [None] * (ROWS // 8)
-        for groups in (range(8), range(8, 16), range(16, 24)):
+        for groups in (range(12), range(12, 24)):
             for n in range(COLS // LANES):
                 value = x_rows[n % 3, pl.ds(col * (PAIRS // 2) + n // 3, 1), :]
                 wide = jnp.broadcast_to(value, (8, LANES))

time: 37.9 us -> 38 us (level)
  no operation moved by 1% of the time
where the time goes in v7:
time: 38 us; the launch traced here: 37.9 us
  Pallas kernels  37.3 us (98%)
  between operations  0.64 us (2%)
    pallas_call x1, Pallas kernels, local(): pl.pallas_call(kernel, out_shape=pltpu.VMEM((8, LANES), jnp.float32), in_...  36.7 us

profile of v7, /device:TPU:1, one launch (start us, length us, event | category | flops | bytes accessed | tf_op | source)
XLA Modules:
  0.0 37.9 jit_solution(5641582144900848688)
XLA Ops:
  0.6 36.7 %shard_map.50.packed = f32[8,128]{1,0:T(8,128)S(1)} custom-call(f32[192,6144]{1,0:T(8,128)} %matrix.1, f32[1,96]{1,0:T(1,128)} %bitcast.2, f32[1,96]{1,0:T(1,128)} %bitcast.3), custom_call_target="tpu_custom_call" | custom-call | tf_op jit(solution)/shard_map/pallas_call | solution.py:207
  37.3 0.6 %shard_map.51 = (f32[4,96]{1,0:T(4,128)}, f32[2,3]{1,0:T(2,128)}) custom-call(f32[8,128]{1,0:T(8,128)S(1)} %shard_map.50.packed), custom_call_target="tpu_custom_call" | custom-call | tf_op jit(solution)/shard_map/pallas_call | solution.py:226

commit v8 on v7

--- a/solution.py
+++ b/solution.py
@@ -121,7 +121,7 @@
     def multiply(diag):
         own = own_rows()
         acc = [None] * (ROWS // 8)
-        for groups in (range(12), range(12, 24)):
+        for groups in (range(16), range(16, 24)):
             for n in range(COLS // LANES):
                 value = x_rows[n % 3, pl.ds(col * (PAIRS // 2) + n // 3, 1), :]
                 wide = jnp.broadcast_to(value, (8, LANES))

time: 38 us -> 37.9 us (level)
  no operation moved by 1% of the time
where the time goes in v8:
time: 37.9 us; the launch traced here: 37.8 us
  Pallas kernels  37.2 us (98%)
  between operations  0.64 us (2%)
    pallas_call x1, Pallas kernels, local(): pl.pallas_call(kernel, out_shape=pltpu.VMEM((8, LANES), jnp.float32), in_...  36.6 us

profile of v8, /device:TPU:1, one launch (start us, length us, event | category | flops | bytes accessed | tf_op | source)
XLA Modules:
  0.0 37.8 jit_solution(14278612226515929076)
XLA Ops:
  0.6 36.6 %shard_map.50.packed = f32[8,128]{1,0:T(8,128)S(1)} custom-call(f32[192,6144]{1,0:T(8,128)} %matrix.1, f32[1,96]{1,0:T(1,128)} %bitcast.2, f32[1,96]{1,0:T(1,128)} %bitcast.3), custom_call_target="tpu_custom_call" | custom-call | tf_op jit(solution)/shard_map/pallas_call | solution.py:207
  37.2 0.6 %shard_map.51 = (f32[4,96]{1,0:T(4,128)}, f32[2,3]{1,0:T(2,128)}) custom-call(f32[8,128]{1,0:T(8,128)S(1)} %shard_map.50.packed), custom_call_target="tpu_custom_call" | custom-call | tf_op jit(solution)/shard_map/pallas_call | solution.py:226
